TPU v7x, 8 devices: a whole 2x2x1 slice. The times are simulated.
8 devices in a mesh: ep: 8 (over z, y, x, core).
Axes of the slice: x: 2, y: 2, z: 1, core: 2. Of those that a mesh axis runs over, the one named last changes fastest.
Arguments:
- x_in: bfloat16 [4096, 3584], P('ep')
- route_idx: int32 [4096, 8], P('ep')
- gate_w: bfloat16 [4096, 8], P('ep')
- dy_in: bfloat16 [4096, 3584], P('ep')
- w_gate: bfloat16 [8, 3584, 2560], P('ep')
- w_up: bfloat16 [8, 3584, 2560], P('ep')
- w_down: bfloat16 [8, 2560, 3584], P('ep')
- hot_gate: bfloat16 [3584, 2560], replicated
- hot_up: bfloat16 [3584, 2560], replicated
- hot_down: bfloat16 [2560, 3584], replicated
Outputs:
- output 1: bfloat16 [4096, 3584], P('ep')
- output 2: bfloat16 [4096, 3584], P('ep')
- output 3: float32 [8, 3584, 2560], P('ep')
- output 4: float32 [8, 3584, 2560], P('ep')
- output 5: float32 [8, 2560, 3584], P('ep')
- output 6: float32 [3584, 2560], P(None, 'ep')
- output 7: float32 [3584, 2560], P(None, 'ep')
- output 8: float32 [2560, 3584], P('ep')
All inputs are finite; a program needn't handle non-finite values.
Results may differ from a plain program's by a relative error of at most 0.0018.
Values are sent between devices in bfloat16 or wider.
A program may use at most 1 GiB of HBM per device.

v0:
```python
import jax
import jax.numpy as jnp
from jax import lax
from jax.sharding import PartitionSpec as P, NamedSharding


def silu_parts(pre_gate):
    sig_val = jax.nn.sigmoid(pre_gate)
    return pre_gate * sig_val, sig_val * (1.0 + pre_gate * (1.0 - sig_val))


def gather_rows(rows, index):
    return jnp.take(rows, index, axis=0, mode='fill', fill_value=0)


def slot_tables(route_loc, experts, slot_cap, hot_cap):
    flat_ids = route_loc.reshape(-1)
    n_assign = flat_ids.shape[0]
    one_hot = (flat_ids[:, None] == jnp.arange(experts + 1, dtype=jnp.int32)[None, :]).astype(jnp.int32)
    rank = jnp.sum((jnp.cumsum(one_hot, axis=0) - 1) * one_hot, axis=1)
    is_hot = flat_ids == experts
    n_regular = experts * slot_cap
    dest = jnp.where(is_hot, n_regular + rank, flat_ids * slot_cap + rank)
    assign_ids = jnp.arange(n_assign, dtype=jnp.int32)
    src_reg = jnp.full((n_regular,), n_assign, jnp.int32).at[jnp.where(is_hot, n_regular, dest)].set(assign_ids, mode='drop')
    src_hot = jnp.full((hot_cap,), n_assign, jnp.int32).at[jnp.where(is_hot, rank, hot_cap)].set(assign_ids, mode='drop')
    return dest, src_reg, src_hot


def scaled_grads(gate_rows, dy_rows):
    product = gate_rows.astype(jnp.float32)[:, :, None] * dy_rows.astype(jnp.float32)[:, None, :]
    return product.astype(jnp.bfloat16).reshape(-1, dy_rows.shape[-1])


def expert_forward(x_rows, gate_mat, up_mat, down_mat):
    u_val = jnp.dot(x_rows, gate_mat, preferred_element_type=jnp.float32)
    v_val = jnp.dot(x_rows, up_mat, preferred_element_type=jnp.float32)
    silu_val, silu_grad = silu_parts(u_val)
    hidden = (silu_val * v_val).astype(jnp.bfloat16)
    result = jnp.dot(hidden, down_mat, preferred_element_type=jnp.float32)
    return result, (x_rows, v_val, silu_val, silu_grad, hidden)


def expert_backward(saved, d_rows, gate_mat, up_mat, down_mat):
    x_rows, v_val, silu_val, silu_grad, hidden = saved
    contract_last = (((1,), (1,)), ((), ()))
    contract_first = (((0,), (0,)), ((), ()))
    grad_hidden = lax.dot_general(d_rows, down_mat, contract_last, preferred_element_type=jnp.float32)
    grad_hidden = grad_hidden.astype(jnp.bfloat16).astype(jnp.float32)
    grad_u = (grad_hidden * v_val * silu_grad).astype(jnp.bfloat16)
    grad_v = (grad_hidden * silu_val).astype(jnp.bfloat16)
    grad_x = (lax.dot_general(grad_u, gate_mat, contract_last, preferred_element_type=jnp.float32) + lax.dot_general(grad_v, up_mat, contract_last, preferred_element_type=jnp.float32))
    grad_gate = lax.dot_general(x_rows, grad_u, contract_first, preferred_element_type=jnp.float32)
    grad_up = lax.dot_general(x_rows, grad_v, contract_first, preferred_element_type=jnp.float32)
    grad_down = lax.dot_general(hidden, d_rows, contract_first, preferred_element_type=jnp.float32)
    return grad_x, grad_gate, grad_up, grad_down


def solution(mesh):
    n_dev = mesh.shape['ep']

    def local_step(x_loc, route_loc, gate_loc, dy_loc, w_gate, w_up, w_down, hot_gate, hot_up, hot_down):
        tok_rows, top_k = route_loc.shape
        d_model = x_loc.shape[1]
        slot_cap = min(tok_rows, 2 * tok_rows * top_k // n_dev)
        hot_cap = 3 * tok_rows // 4
        dest, src_reg, src_hot = slot_tables(route_loc, n_dev, slot_cap, hot_cap)
        x_recv = lax.all_to_all(gather_rows(x_loc, src_reg // top_k), 'ep', 0, 0, tiled=True)
        out_reg, saved_reg = expert_forward(x_recv, w_gate[0], w_up[0], w_down[0])
        out_back = lax.all_to_all(out_reg.astype(jnp.bfloat16), 'ep', 0, 0, tiled=True)
        out_hot, saved_hot = expert_forward(gather_rows(x_loc, src_hot // top_k), hot_gate, hot_up, hot_down)
        out_all = jnp.concatenate([out_back, out_hot.astype(jnp.bfloat16)], axis=0)
        out_assign = gather_rows(out_all, dest).reshape(tok_rows, top_k, d_model)
        y_loc = jnp.einsum('tk,tkd->td', gate_loc, out_assign, preferred_element_type=jnp.float32).astype(jnp.bfloat16)
        d_assign = scaled_grads(gate_loc, dy_loc)
        d_recv = lax.all_to_all(gather_rows(d_assign, src_reg), 'ep', 0, 0, tiled=True)
        dx_reg, grad_gate, grad_up, grad_down = expert_backward(saved_reg, d_recv, w_gate[0], w_up[0], w_down[0])
        dx_back = lax.all_to_all(dx_reg.astype(jnp.bfloat16), 'ep', 0, 0, tiled=True)
        dx_hot, hot_dgate, hot_dup, hot_ddown = expert_backward(saved_hot, gather_rows(d_assign, src_hot), hot_gate, hot_up, hot_down)
        dx_all = jnp.concatenate([dx_back, dx_hot.astype(jnp.bfloat16)], axis=0)
        dx_assign = gather_rows(dx_all, dest).reshape(tok_rows, top_k, d_model)
        dx_loc = jnp.sum(dx_assign, axis=1, dtype=jnp.float32).astype(jnp.bfloat16)
        hot_dgate = lax.psum_scatter(hot_dgate, 'ep', scatter_dimension=1, tiled=True)
        hot_dup = lax.psum_scatter(hot_dup, 'ep', scatter_dimension=1, tiled=True)
        hot_ddown = lax.psum_scatter(hot_ddown, 'ep', scatter_dimension=0, tiled=True)
        return (y_loc, dx_loc, grad_gate[None], grad_up[None], grad_down[None], hot_dgate, hot_dup, hot_ddown)

    row_spec = P('ep', None)
    expert_spec = P('ep', None, None)
    whole_spec = P(None, None)
    return jax.shard_map(local_step, mesh=mesh, in_specs=(row_spec, row_spec, row_spec, row_spec, expert_spec, expert_spec, expert_spec, whole_spec, whole_spec, whole_spec), out_specs=(row_spec, row_spec, expert_spec, expert_spec, expert_spec, P(None, 'ep'), P(None, 'ep'), P('ep', None)), check_vma=False)
```

profile of v0, /device:TPU:0, one launch (start us, length us, event | category | flops | bytes accessed | tf_op | source)
XLA Modules:
  0.0 2438.5 jit_solution(8234218585958348665)
XLA Ops:
  7.2 0.7 broadcast_compare_fusion
  7.9 0.7 broadcast_multiply_fusion
  8.7 0.8 copy.18
  9.5 0.1 eq.52
  9.8 0.2 copy.20
  10.0 0.2 eq.51
  10.3 0.2 mul.88
  10.5 2.6 reduce-window.6
  13.1 0.3 slice_reduce_fusion
  13.4 0.2 reduce-window.9
  13.8 0.2 copy.25
  14.0 0.6 copy-done.10
  14.7 15.5 scatter_custom_fusion.1
  30.3 0.8 copy.22
  31.1 0.1 reshape.165
  31.3 6.0 convert_element_type.66
  37.3 9.6 gather_fusion.1
  46.9 12.6 fusion
  59.5 19.0 gather_fusion.3
  78.5 13.3 fusion.42
  91.7 11.2 convolution_convert_fusion.3
  103.0 1.3 copy-done.5
  104.2 19.6 fusion.39
  123.9 13.9 fusion.21
  137.8 1.3 copy-done.6
  139.0 16.7 fusion.40
  155.8 15.7 scatter_custom_fusion
  171.6 63.9 %gather_fusion.2 = bf16[4096,3584]{1,0:T(8,128)(2,1)} fusion(bf16[4096,3584]{1,0:T(8,128)(2,1)} %fusion, s32[4096]{0:T(1024)S(1)} %get-tuple-element.19), kind=kCustom, calls=%fused_computation.4 | custom fusion | bytes 58736640 | tf_op jit(solution)/shard_map/jit(_take)/gather | solution.py:13
  235.5 20.5 broadcast_select_fusion
  255.9 5.8 all-to-all-start.2
  261.7 0.3 reduce-scatter.8.cloned.1.call-start
  262.0 18.5 fusion.24
  280.6 0.6 copy-done.14
  281.3 0.9 copy.23
  282.1 53.2 %gather_fusion = bf16[4096,3584]{1,0:T(8,128)(2,1)} fusion(bf16[512,3584]{1,0:T(8,128)(2,1)} %param.12, s32[4096]{0:T(1024)S(1)} %get-tuple-element.20), kind=kCustom, calls=%fused_computation.2 | custom fusion | bytes 58736640 | tf_op jit(solution)/shard_map/jit(_take)/gather | solution.py:13
  335.4 0.6 compare_and_fusion
  336.0 0.6 broadcast_clamp_fusion
  336.6 20.5 broadcast_select_fusion.1
  357.0 334.4 %all-to-all-done.2 = bf16[8,512,3584]{2,1,0:T(8,128)(2,1)} async-done(((bf16[8,512,3584]{2,1,0:T(8,128)(2,1)}), bf16[8,512,3584]{2,1,0:T(8,128)(2,1)}, u32[]{:S(2)}, u32[]{:S(2)}) %all-to-all-start.2) | async-done | bytes 29360160 | tf_op jit(solution)/shard_map/all_to_all | solution.py:76
  691.4 5.9 all-to-all-start
  697.3 12.6 fusion.47
  710.0 15.9 fusion.19
  725.9 12.1 convolution_convert_fusion.2
  738.0 85.1 %convolution_convert_fusion.1 = bf16[4096,2560]{1,0:T(8,128)(2,1)} fusion(bf16[4096,3584]{1,0:T(8,128)(2,1)} %bitcast.16, bf16[1,2560,3584]{2,1,0:T(8,128)(2,1)} %param.18), kind=kOutput, calls=%fused_computation.32 | convolution fusion | flops 75172413440 | bytes 68681728 | tf_op jit(solution)/shard_map/dot_general | solution.py:48
  823.1 283.8 %all-to-all-done = bf16[8,512,3584]{2,1,0:T(8,128)(2,1)} async-done(((bf16[8,512,3584]{2,1,0:T(8,128)(2,1)}), bf16[8,512,3584]{2,1,0:T(8,128)(2,1)}, u32[]{:S(2)}, u32[]{:S(2)}) %all-to-all-start) | async-done | bytes 29360160 | tf_op jit(solution)/shard_map/all_to_all | solution.py:68
  1106.9 85.2 %fusion.16 = f32[4096,2560]{1,0:T(8,128)} fusion(bf16[4096,3584]{1,0:T(8,128)(2,1)} %bitcast.4, bf16[1,3584,2560]{2,1,0:T(8,128)(2,1)} %param.16), kind=kOutput, calls=%fused_computation.40 | convolution fusion | flops 75161927680 | bytes 89653248 | tf_op jit(solution)/shard_map/dot_general | solution.py:36
  1192.1 100.8 %fusion.2 = (bf16[4096,2560]{1,0:T(8,128)(2,1)}, bf16[4096,2560]{1,0:T(8,128)(2,1)}) fusion(bf16[4096,2560]{1,0:T(8,128)(2,1)} %convolution_convert_fusion.1, f32[4096,2560]{1,0:T(8,128)} %fusion.16, bf16[4096,3584]{1,0:T(8,128)(2,1)} %bitcast.4, bf16[1,3584,2560]{2,1,0:T(8,128)(2,1)} %param.17), kind=kOutput, calls=%fused_computation.14 | convolution fusion | flops 75308728320 | bytes 152567808 | tf_op jit(solution)/shard_map/dot_general | solution.py:37
  1293.0 87.6 %convolution_bitcast_fusion.2 = f32[1,3584,2560]{2,1,0:T(8,128)} fusion(bf16[4096,3584]{1,0:T(8,128)(2,1)} %bitcast.4, bf16[4096,2560]{1,0:T(8,128)(2,1)} %get-tuple-element.11), kind=kOutput, calls=%fused_computation.31 | convolution fusion | flops 75161927680 | bytes 87031808 | tf_op jit(solution)/shard_map/dot_general | solution.py:53
  1380.6 86.1 %fusion.14 = f32[4096,3584]{1,0:T(8,128)} fusion(bf16[4096,2560]{1,0:T(8,128)(2,1)} %get-tuple-element.11, bf16[1,3584,2560]{2,1,0:T(8,128)(2,1)} %param.16), kind=kOutput, calls=%fused_computation.38 | convolution fusion | flops 75161927680 | bytes 98041856 | tf_op jit(solution)/shard_map/dot_general | solution.py:52
  1466.7 84.1 %convolution_convert_fusion = bf16[4096,3584]{1,0:T(8,128)(2,1)} fusion(bf16[4096,2560]{1,0:T(8,128)(2,1)} %get-tuple-element.12, bf16[1,2560,3584]{2,1,0:T(8,128)(2,1)} %param.18), kind=kOutput, calls=%fused_computation.21 | convolution fusion | flops 75176607744 | bytes 68681728 | tf_op jit(solution)/shard_map/dot_general | solution.py:40
  1550.8 5.7 all-to-all-start.1
  1556.5 28.5 %fusion.75 = bf16[4096,2560]{1,0:T(8,128)(2,1)} fusion(bf16[4096,2560]{1,0:T(8,128)(2,1)} %convolution_convert_fusion.1, f32[4096,2560]{1,0:T(8,128)} %fusion.16), kind=kLoop, calls=%fused_computation.15.clone.1.clone.1 | loop fusion | flops 73400320 | bytes 83886080 | tf_op jit(solution)/shard_map/dot_general | solution.py:52
  1585.0 90.6 %add_convert_fusion = bf16[4096,3584]{1,0:T(8,128)(2,1)} fusion(f32[4096,3584]{1,0:T(8,128)} %fusion.14, bf16[1,3584,2560]{2,1,0:T(8,128)(2,1)} %param.17, bf16[4096,2560]{1,0:T(8,128)(2,1)} %fusion.75), kind=kOutput, calls=%fused_computation.10 | convolution fusion | flops 75191287808 | bytes 127401984 | tf_op jit(solution)/shard_map/dot_general | solution.py:52
  1675.6 199.8 %all-to-all-done.1 = bf16[8,512,3584]{2,1,0:T(8,128)(2,1)} async-done(((bf16[8,512,3584]{2,1,0:T(8,128)(2,1)}), bf16[8,512,3584]{2,1,0:T(8,128)(2,1)}, u32[]{:S(2)}, u32[]{:S(2)}) %all-to-all-start.1) | async-done | bytes 29360160 | tf_op jit(solution)/shard_map/all_to_all | solution.py:70
  1875.4 5.8 all-to-all-start.3
  1881.2 87.3 %convolution_bitcast_fusion = f32[1,2560,3584]{2,1,0:T(8,128)} fusion(bf16[4096,2560]{1,0:T(8,128)(2,1)} %get-tuple-element.12, bf16[4096,3584]{1,0:T(8,128)(2,1)} %bitcast.16), kind=kOutput, calls=%fused_computation.29 | convolution fusion | flops 75161927680 | bytes 87031808 | tf_op jit(solution)/shard_map/dot_general | solution.py:55
  1968.5 115.0 %convolution_bitcast_fusion.1 = f32[1,3584,2560]{2,1,0:T(8,128)} fusion(bf16[4096,3584]{1,0:T(8,128)(2,1)} %bitcast.4, bf16[4096,2560]{1,0:T(8,128)(2,1)} %convolution_convert_fusion.1, f32[4096,2560]{1,0:T(8,128)} %fusion.16), kind=kOutput, calls=%fused_computation.30 | convolution fusion | flops 75235328000 | bytes 128974848 | tf_op jit(solution)/shard_map/dot_general | solution.py:54
  2083.4 27.0 %pad_maximum_fusion = bf16[4480,3584]{1,0:T(8,128)(2,1)} fusion(bf16[384,3584]{1,0:T(8,128)(2,1)S(1)} %copy-done.3, bf16[4096,3584]{1,0:T(8,128)(2,1)} %bitcast.9), kind=kLoop, calls=%fused_computation.19 | loop fusion | flops 64225280 | bytes 64225280 | tf_op jit(solution)/shard_map/concatenate | solution.py:72
  2110.5 123.4 %gather_fusion.4 = bf16[4096,3584]{1,0:T(8,128)(2,1)} fusion(bf16[4480,3584]{1,0:T(8,128)(2,1)} %pad_maximum_fusion, s32[4096]{0:T(1024)S(1)} %copy-done.13), kind=kCustom, calls=%fused_computation.clone | custom fusion | bytes 58736640 | tf_op jit(solution)/shard_map/jit(_take)/gather | solution.py:13
  2233.9 15.5 fusion.5
  2249.4 5.7 copy.27
  2255.1 27.3 %pad_maximum_fusion.1 = bf16[4480,3584]{1,0:T(8,128)(2,1)} fusion(bf16[384,3584]{1,0:T(8,128)(2,1)S(1)} %copy-done.2, bf16[4096,3584]{1,0:T(8,128)(2,1)} %bitcast.18), kind=kLoop, calls=%fused_computation.20 | loop fusion | flops 64225280 | bytes 64225280 | tf_op jit(solution)/shard_map/concatenate | solution.py:80
  2282.4 123.5 %gather_fusion.5 = bf16[4096,3584]{1,0:T(8,128)(2,1)} fusion(bf16[4480,3584]{1,0:T(8,128)(2,1)} %pad_maximum_fusion.1, s32[4096]{0:T(1024)S(1)} %copy-done.13), kind=kCustom, calls=%fused_computation.1.clone | custom fusion | bytes 58736640 | tf_op jit(solution)/shard_map/jit(_take)/gather | solution.py:13
  2405.9 25.5 %bitcast_reduce_fusion = bf16[512,3584]{1,0:T(8,128)(2,1)} fusion(bf16[4096,3584]{1,0:T(8,128)(2,1)} %gather_fusion.5, pred[4096]{0:T(1024)(128)(4,1)S(1)} %copy-done.15), kind=kLoop, calls=%fused_computation.22 | loop fusion | flops 27525120 | bytes 33034240 | tf_op jit(solution)/shard_map/reduce_sum | solution.py:82
  (58 shorter events, 0.9 us)
Async XLA Ops:
  7.2 2424.3 %reduce-scatter.6.cloned.1.call-start = ((), (), s32[]{:S(2)}) async-start(), calls=%async_computation.8 | async-start | bytes 41287680 | tf_op jit(solution)/shard_map/reduce_scatter | solution.py:84
  9.7 21.6 copy-start.8
  14.0 0.6 copy-start.10
  30.2 61.5 %copy-start.16 = (pred[384]{0:T(512)(128)(4,1)}, pred[384]{0:T(512)(128)(4,1)S(1)}, u32[]{:S(2)}) copy-start(pred[384]{0:T(512)(128)(4,1)S(1)} %get-tuple-element.21) | copy-start | bytes 1156
  78.5 13.3 copy-start
  102.9 1.3 copy-start.5
  123.8 2307.6 %reduce-scatter.4.cloned.1.call-start = ((), (), s32[]{:S(2)}) async-start(), calls=%async_computation.7 | async-start | bytes 41287680 | tf_op jit(solution)/shard_map/reduce_scatter | solution.py:83
  137.7 1.3 copy-start.6
  255.9 6.1 copy-start.1
  255.9 6.1 copy-start.17
  255.9 435.5 %all-to-all-start.2 = ((bf16[8,512,3584]{2,1,0:T(8,128)(2,1)}), bf16[8,512,3584]{2,1,0:T(8,128)(2,1)}, u32[]{:S(2)}, u32[]{:S(2)}) async-start(bf16[8,512,3584]{2,1,0:T(8,128)(2,1)} %broadcast_select_fusion), calls=%async_computation.2 | async-start | bytes 58720256 | tf_op jit(solution)/shard_map/all_to_all | solution.py:76
  261.7 2169.7 %reduce-scatter.8.cloned.1.call-start = ((), (), s32[]{:S(2)}) async-start(), calls=%async_computation.9 | async-start | bytes 41287680 | tf_op jit(solution)/shard_map/reduce_scatter | solution.py:85
  280.6 0.7 copy-start.14
  282.1 53.3 %copy-start.9 = (s32[4096]{0:T(1024)S(1)}, s32[4096]{0:T(1024)}, u32[]{:S(2)}) copy-start(s32[4096]{0:T(1024)} %copy-done.8) | copy-start | bytes 49156
  282.1 53.3 %copy-start.11 = (s32[4096]{0:T(1024)S(1)}, s32[4096]{0:T(1024)}, u32[]{:S(2)}) copy-start(s32[4096]{0:T(1024)} %copy-done.10) | copy-start | bytes 49156
  357.0 340.3 %copy-start.7 = (bf16[384,2560]{1,0:T(8,128)(2,1)S(1)}, bf16[384,2560]{1,0:T(8,128)(2,1)}, u32[]{:S(2)}) copy-start(bf16[384,2560]{1,0:T(8,128)(2,1)} %copy-done.6) | copy-start | bytes 5898244
  691.4 415.5 %all-to-all-start = ((bf16[8,512,3584]{2,1,0:T(8,128)(2,1)}), bf16[8,512,3584]{2,1,0:T(8,128)(2,1)}, u32[]{:S(2)}, u32[]{:S(2)}) async-start(bf16[8,512,3584]{2,1,0:T(8,128)(2,1)} %broadcast_select_fusion.1), calls=%async_computation | async-start | bytes 58720256 | tf_op jit(solution)/shard_map/all_to_all | solution.py:68
  710.0 15.9 copy-start.4
  1550.8 324.6 %all-to-all-start.1 = ((bf16[8,512,3584]{2,1,0:T(8,128)(2,1)}), bf16[8,512,3584]{2,1,0:T(8,128)(2,1)}, u32[]{:S(2)}, u32[]{:S(2)}) async-start(bf16[8,512,3584]{2,1,0:T(8,128)(2,1)} %bitcast.85), calls=%async_computation.1 | async-start | bytes 58720256 | tf_op jit(solution)/shard_map/all_to_all | solution.py:70
  1875.4 379.7 %all-to-all-start.3 = ((bf16[8,512,3584]{2,1,0:T(8,128)(2,1)}), bf16[8,512,3584]{2,1,0:T(8,128)(2,1)}, u32[]{:S(2)}, u32[]{:S(2)}) async-start(bf16[8,512,3584]{2,1,0:T(8,128)(2,1)} %bitcast.84), calls=%async_computation.3 | async-start | bytes 58720256 | tf_op jit(solution)/shard_map/all_to_all | solution.py:78
  1968.5 115.0 %copy-start.3 = (bf16[384,3584]{1,0:T(8,128)(2,1)S(1)}, bf16[384,3584]{1,0:T(8,128)(2,1)}, u32[]{:S(2)}) copy-start(bf16[384,3584]{1,0:T(8,128)(2,1)} %convolution_convert_fusion.2) | copy-start | bytes 8257540
  2083.4 27.0 %copy-start.13 = (s32[4096]{0:T(1024)S(1)}, s32[4096]{0:T(1024)}, u32[]{:S(2)}) copy-start(s32[4096]{0:T(1024)} %broadcast_clamp_fusion) | copy-start | bytes 49156
  2110.5 123.4 %copy-start.12 = (bf16[512,8,1]{1,2,0:T(2,128)(2,1)S(1)}, bf16[512,8,1]{1,2,0:T(2,128)(2,1)}, u32[]{:S(2)}) copy-start(bf16[512,8,1]{1,2,0:T(2,128)(2,1)} %copy.23) | copy-start | bytes 24580
  2110.5 123.4 %copy-start.15 = (pred[4096]{0:T(1024)(128)(4,1)S(1)}, pred[4096]{0:T(1024)(128)(4,1)}, u32[]{:S(2)}) copy-start(pred[4096]{0:T(1024)(128)(4,1)} %compare_and_fusion) | copy-start | bytes 12292
  2233.9 21.2 copy-start.2
Sparse Core Ops, SparseCore 0:
  124.0 413.6 reduce-scatter.5
  541.9 458.0 reduce-scatter.3
  1004.2 257.9 reduce-scatter.7
where the time goes:
time: 2450 us; the launch traced here: 2440 us
  matrix products  971 us (40%)
  waiting for transfers between devices  818 us (33%)
  local copies, waits for them, and re-layouts  437 us (18%)
  other arithmetic  174 us (7%)
    gather x6, local copies, waits for them, and re-layouts, gather_rows(): return jnp.take(rows, index, axis=0, mode='fill', fill_value=0)  393 us
    all_to_all x1, waiting for transfers between devices, local_step(): lax.all_to_all(gather_rows(d_assign, src_reg), 'ep', 0, 0, tiled=True)  334 us
    all_to_all x1, waiting for transfers between devices, local_step(): lax.all_to_all(gather_rows(x_loc, src_reg // top_k), 'ep', 0, 0, tiled=True)  284 us
    all_to_all x1, waiting for transfers between devices, local_step(): lax.all_to_all(out_reg.astype(jnp.bfloat16), 'ep', 0, 0, tiled=True)  200 us
    dot_general x2, matrix products, expert_backward(): lax.dot_general(x_rows, grad_v, contract_first, preferred_element_type=jn...  135 us
    dot_general x2, matrix products, expert_forward(): v_val = jnp.dot(x_rows, up_mat, preferred_element_type=jnp.float32)  115 us
    dot_general x2, matrix products, expert_backward(): lax.dot_general(grad_v, up_mat, contract_last, preferred_element_type=jnp...  107 us
    dot_general x2, matrix products, expert_backward(): lax.dot_general(hidden, d_rows, contract_first, preferred_element_type=jn...  106 us
  transfers between devices with their start and end apart: 7, of which 3 were waited for; matrix products, arithmetic and copies ran while one was open for 60% of the time, Pallas kernels for 0%

commit v1 on v0

v1 whole, which is shorter than its diff:
```python
import jax
import jax.numpy as jnp
from jax import lax
from jax.sharding import PartitionSpec as P

F32 = jnp.float32
BF16 = jnp.bfloat16
CONTRACT_LAST = (((1,), (1,)), ((), ()))
CONTRACT_FIRST = (((0,), (0,)), ((), ()))


def mm(a, b):
    return jnp.dot(a, b, preferred_element_type=F32)


def mm_last(a, b):
    return lax.dot_general(a, b, CONTRACT_LAST, preferred_element_type=F32)


def mm_first(a, b):
    return lax.dot_general(a, b, CONTRACT_FIRST, preferred_element_type=F32)


def rounded(value):
    return lax.reduce_precision(value, exponent_bits=8, mantissa_bits=7)


def silu_parts(pre_gate):
    sig_val = jax.nn.sigmoid(pre_gate)
    return pre_gate * sig_val, sig_val * (1.0 + pre_gate * (1.0 - sig_val))


def dense_gates(route_loc, gate_loc, n_choice):
    hit = route_loc[:, :, None] == jnp.arange(n_choice, dtype=jnp.int32)[None, None, :]
    gates = jnp.sum(jnp.where(hit, gate_loc.astype(F32)[:, :, None], 0.0), axis=1)
    return gates, jnp.any(hit, axis=1)


def hidden_of(u_val, v_val, keep):
    silu_val, _ = silu_parts(u_val)
    return jnp.where(keep, silu_val * v_val, 0.0).astype(BF16)


def hidden_grads(u_val, v_val, grad_hidden, keep):
    silu_val, silu_grad = silu_parts(u_val)
    p_val = rounded(grad_hidden)
    du = jnp.where(keep, p_val * v_val * silu_grad, 0.0).astype(BF16)
    dv = jnp.where(keep, p_val * silu_val, 0.0).astype(BF16)
    return du, dv


def solution(mesh):
    n_dev = mesh.shape['ep']

    def local_step(x_loc, route_loc, gate_loc, dy_loc, w_gate, w_up, w_down, hot_gate, hot_up, hot_down):
        me = lax.axis_index('ep')
        tok, d_model = x_loc.shape
        d_ff = hot_gate.shape[1]
        part = d_ff // n_dev
        w_gate, w_up, w_down = w_gate[0], w_up[0], w_down[0]

        gates, chosen = dense_gates(route_loc, gate_loc, n_dev + 1)
        table = jnp.concatenate([gates, chosen.astype(F32)], axis=1)
        table_all = lax.all_gather(table, 'ep', axis=0, tiled=True)
        gates_all, chosen_all = table_all[:, :n_dev + 1], table_all[:, n_dev + 1:]
        mine = (jnp.arange(n_dev + 1, dtype=jnp.int32) == me)[None, :]
        g_mine = jnp.sum(jnp.where(mine, gates_all, 0.0), axis=1, keepdims=True)
        keep_mine = jnp.sum(jnp.where(mine, chosen_all, 0.0), axis=1, keepdims=True) > 0.5
        g_hot, keep_hot = gates_all[:, n_dev:], chosen_all[:, n_dev:] > 0.5
        g_hot_loc, keep_hot_loc = gates[:, n_dev:], chosen[:, n_dev:]

        x_all = lax.all_gather(x_loc, 'ep', axis=0, tiled=True)
        dy_all = lax.all_gather(dy_loc, 'ep', axis=0, tiled=True)

        uh = mm(x_loc, hot_gate)
        vh = mm(x_loc, hot_up)
        oh = mm(hidden_of(uh, vh, keep_hot_loc), hot_down)
        y_hot = g_hot_loc * rounded(oh)
        qh = (g_hot_loc * dy_loc.astype(F32)).astype(BF16)
        duh, dvh = hidden_grads(uh, vh, mm_last(qh, hot_down), keep_hot_loc)
        dx_hot = rounded(mm_last(duh, hot_gate) + mm_last(dvh, hot_up))

        x_all, y_hot, dx_hot = lax.optimization_barrier((x_all, y_hot, dx_hot))

        u_val = mm(x_all, w_gate)
        v_val = mm(x_all, w_up)
        hidden = hidden_of(u_val, v_val, keep_mine)
        out = g_mine * rounded(mm(hidden, w_down))
        y_sum = lax.psum_scatter(out, 'ep', scatter_dimension=0, tiled=True)
        q_mine = (g_mine * dy_all.astype(F32)).astype(BF16)
        du, dv = hidden_grads(u_val, v_val, mm_last(q_mine, w_down), keep_mine)
        r_val = rounded(mm_last(du, w_gate) + mm_last(dv, w_up))
        dx_sum = lax.psum_scatter(r_val, 'ep', scatter_dimension=0, tiled=True)
        grad_gate = mm_first(x_all, du)
        grad_up = mm_first(x_all, dv)
        grad_down = mm_first(hidden, q_mine)

        hg = lax.dynamic_slice_in_dim(hot_gate, me * part, part, axis=1)
        hu = lax.dynamic_slice_in_dim(hot_up, me * part, part, axis=1)
        hd = lax.dynamic_slice_in_dim(hot_down, me * part, part, axis=0)
        uv = mm(x_all, jnp.concatenate([hg, hu], axis=1))
        us, vs = uv[:, :part], uv[:, part:]
        q_hot = (g_hot * dy_all.astype(F32)).astype(BF16)
        dus, dvs = hidden_grads(us, vs, mm_last(q_hot, hd), keep_hot)
        hot_duv = mm_first(x_all, jnp.concatenate([dus, dvs], axis=1))
        hot_ddown = mm_first(hidden_of(us, vs, keep_hot), q_hot)

        y_loc = (y_sum + y_hot).astype(BF16)
        dx_loc = (dx_sum + dx_hot).astype(BF16)
        return (y_loc, dx_loc, grad_gate[None], grad_up[None], grad_down[None], hot_duv[:, :part], hot_duv[:, part:], hot_ddown)

    row_spec = P('ep', None)
    expert_spec = P('ep', None, None)
    whole_spec = P(None, None)
    return jax.shard_map(local_step, mesh=mesh, in_specs=(row_spec, row_spec, row_spec, row_spec, expert_spec, expert_spec, expert_spec, whole_spec, whole_spec, whole_spec), out_specs=(row_spec, row_spec, expert_spec, expert_spec, expert_spec, P(None, 'ep'), P(None, 'ep'), P('ep', None)), check_vma=False)
```

time: 2450 us -> 1170 us (0.48)
  waiting for transfers between devices: 818 us -> 73.4 us
  local copies, waits for them, and re-layouts: 437 us -> 16.9 us
  other arithmetic: 174 us -> 20.6 us
  matrix products: 971 us -> 1020 us
    all_to_all x4 -> x0, waiting for transfers between devices: 818 us -> none  [the longest x1 334 us: local_step(): lax.all_to_all(gather_rows(d_assign, src_reg), 'ep', 0, 0, tiled=True)]
    gather x6 -> x0, local copies, waits for them, and re-layouts: 393 us -> none  [gather_rows(): return jnp.take(rows, index, axis=0, mode='fill', fill_value=0)]
    reduce_scatter x3 -> x2, waiting for transfers between devices: 0.01 us -> 60.1 us  [the longest x1 60.1 us: local_step(): dx_sum = lax.psum_scatter(r_val, 'ep', scatter_dimension=0, tiled=True)]
    concatenate x2 -> x1, other arithmetic: 54.3 us -> 0.01 us  [local_step(): table = jnp.concatenate([gates, chosen.astype(F32)], axis=1)]
    dot_general x19, matrix products: 971 us -> 1020 us  [the longest x7 368 us: mm_last(): return lax.dot_general(a, b, CONTRACT_LAST, preferred_element_type=F32)]
    select_n x4 -> x0, other arithmetic: 41 us -> none  [the longest x3 40.9 us: gather_rows(): return jnp.take(rows, index, axis=0, mode='fill', fill_value=0)]
    scatter x2 -> x0, local copies, waits for them, and re-layouts: 31.2 us -> none  [the longest x1 15.7 us: slot_tables(): jnp.full((n_regular,), n_assign, jnp.int32)]
    dot_general x1 -> x0, other arithmetic: 28.5 us -> none  [expert_backward(): lax.dot_general(grad_v, up_mat, contract_last, preferred_element_type=jnp...]
  transfers between devices with their start and end apart: 7 -> 4, of which waited for: 3 -> 2; matrix products, arithmetic and copies ran while one was open for 60% -> 74% of each run, Pallas kernels for 0% -> 0%
where the time goes in v1:
time: 1170 us; the launch traced here: 1160 us
  matrix products  1020 us (87%)
  waiting for transfers between devices  73.4 us (6%)
  other arithmetic  20.6 us (2%)
  local copies, waits for them, and re-layouts  16.9 us (1%)
  blocking collectives  15.8 us (1%)
  between operations  14.3 us (1%)
    dot_general x7, matrix products, mm_last(): return lax.dot_general(a, b, CONTRACT_LAST, preferred_element_type=F32)  368 us
    dot_general x7, matrix products, mm(): return jnp.dot(a, b, preferred_element_type=F32)  339 us
    dot_general x5, matrix products, mm_first(): return lax.dot_general(a, b, CONTRACT_FIRST, preferred_element_type=F32)  314 us
    reduce_scatter x1, waiting for transfers between devices, local_step(): dx_sum = lax.psum_scatter(r_val, 'ep', scatter_dimension=0, tiled=True)  60.1 us
  transfers between devices with their start and end apart: 4, of which 2 were waited for; matrix products, arithmetic and copies ran while one was open for 74% of the time, Pallas kernels for 0%

profile of v1, /device:TPU:0, one launch (start us, length us, event | category | flops | bytes accessed | tf_op | source)
XLA Modules:
  0.0 1161.3 jit_solution(12108456817383886205)
XLA Ops:
  7.2 0.0 all-gather.3.cloned.1.call-start
  7.2 0.7 all-gather.3.cloned.1.call-update
  7.9 0.0 all-gather.5.cloned.1.call-start
  7.9 0.7 all-gather.5.cloned.1.call-update
  8.6 0.0 reduce-scatter.3.cloned.1.call-start
  8.7 0.8 fusion.50
  9.5 0.7 convert_element_type.55
  10.2 0.8 select_reduce_fusion
  11.0 15.8 %all_gather.9 = f32[4096,18]{0,1:T(8,128)S(1)} all-gather(f32[512,18]{0,1:T(8,128)S(1)} %pad_maximum_fusion), channel_id=1, replica_groups=mesh['ep'=8] {'ep'}, dimensions={0}, use_global_device_ids=true | all-gather | bytes 331776 | tf_op jit(solution)/shard_map/all_gather | solution.py:64
  26.9 0.0 copy-start.1
  26.9 0.8 fusion.49
  27.7 0.6 broadcast_compare_fusion
  28.3 16.0 %fusion.64 = f32[512,2560]{1,0:T(8,128)} fusion(bf16[512,3584]{1,0:T(8,128)(2,1)} %param.10, bf16[3584,2560]{1,0:T(8,128)(2,1)} %param.18), kind=kOutput, calls=%fused_computation.90 | convolution fusion | flops 9395240960 | bytes 27262976 | tf_op jit(solution)/shard_map/dot_general | solution.py:13
  44.2 0.0 copy-done.1
  44.2 0.0 copy-start
  44.2 16.2 %fusion.32 = f32[512,2560]{1,0:T(8,128)} fusion(bf16[2560,3584]{1,0:T(8,128)(2,1)} %param.19, bf16[512,3584]{1,0:T(8,128)(2,1)} %param.13, f32[512]{0:T(512)S(1)} %bitcast.50), kind=kOutput, calls=%fused_computation.50 | convolution fusion | flops 9400745984 | bytes 27265024 | tf_op jit(solution)/shard_map/dot_general | solution.py:17
  60.5 0.0 copy-done
  60.5 14.9 %fusion.63 = f32[512,2560]{1,0:T(8,128)} fusion(bf16[512,3584]{1,0:T(8,128)(2,1)S(1)} %copy-done, bf16[3584,2560]{1,0:T(8,128)(2,1)} %param.17), kind=kOutput, calls=%fused_computation.89 | convolution fusion | flops 9395240960 | bytes 27262976 | tf_op jit(solution)/shard_map/dot_general | solution.py:13
  75.4 22.6 %fusion.34 = f32[512,3584]{1,0:T(8,128)} fusion(bf16[3584,2560]{1,0:T(8,128)(2,1)} %param.17, f32[512,2560]{1,0:T(8,128)} %fusion.63, f32[512,2560]{1,0:T(8,128)} %fusion.64, f32[512,2560]{1,0:T(8,128)} %fusion.32, pred[512]{0:T(512)(128)(4,1)S(1)} %slice_reduce_fusion), kind=kOutput, calls=%fused_computation.52 | convolution fusion | flops 9410969600 | bytes 41419264 | tf_op jit(solution)/shard_map/dot_general | solution.py:17
  97.9 20.9 %add_reduce-precision_fusion.1 = f32[512,3584]{1,0:T(8,128)} fusion(f32[512,3584]{1,0:T(8,128)} %fusion.34, bf16[3584,2560]{1,0:T(8,128)(2,1)} %param.18, f32[512,2560]{1,0:T(8,128)} %fusion.32, pred[512]{0:T(512)(128)(4,1)S(1)} %slice_reduce_fusion, f32[512,2560]{1,0:T(8,128)} %fusion.63), kind=kOutput, calls=%fused_computation.28 | convolution fusion | flops 9409396736 | bytes 43516416 | tf_op jit(solution)/shard_map/dot_general | solution.py:17
  118.9 19.9 %reduce-precision_multiply_fusion.1 = f32[512,3584]{1,0:T(8,128)} fusion(bf16[2560,3584]{1,0:T(8,128)(2,1)} %param.19, f32[512]{0:T(512)S(1)} %bitcast.51, f32[512,2560]{1,0:T(8,128)} %fusion.64, pred[512]{0:T(512)(128)(4,1)S(1)} %slice_reduce_fusion, f32[512,2560]{1,0:T(8,128)} %fusion.63), kind=kOutput, calls=%fused_computation.30 | convolution fusion | flops 9408086016 | bytes 36178432 | tf_op jit(solution)/shard_map/dot_general | solution.py:13
  138.8 11.8 %all-gather.3.cloned.1.call-done = bf16[4096,3584]{1,0:T(8,128)(2,1)} async-done(((bf16[512,3584]{1,0:T(8,128)(2,1)}), bf16[4096,3584]{1,0:T(8,128)(2,1)}) %all-gather.3.cloned.1.call-update) | async-done | bytes 29360144 | tf_op jit(solution)/shard_map/all_gather | solution.py:72
  150.6 85.0 %fusion.11 = f32[4096,2560]{1,0:T(8,128)} fusion(bf16[4096,3584]{1,0:T(8,128)(2,1)} %all-gather.3.cloned.1.call-done, bf16[1,3584,2560]{2,1,0:T(8,128)(2,1)} %param.14), kind=kOutput, calls=%fused_computation.22 | convolution fusion | flops 75161927680 | bytes 89653248 | tf_op jit(solution)/shard_map/dot_general | solution.py:13
  235.6 0.0 copy-start.2
  235.6 0.0 copy-start.4
  235.6 85.6 %fusion.7 = f32[4096,2560]{1,0:T(8,128)} fusion(bf16[4096,3584]{1,0:T(8,128)(2,1)} %all-gather.3.cloned.1.call-done, bf16[1,3584,2560]{2,1,0:T(8,128)(2,1)} %param.15), kind=kOutput, calls=%fused_computation.18 | convolution fusion | flops 75161927680 | bytes 89653248 | tf_op jit(solution)/shard_map/dot_general | solution.py:13
  321.2 0.0 all-gather.5.cloned.1.call-done
  321.2 0.0 copy-done.2
  321.2 0.0 copy-done.4
  321.2 109.5 %select_convert_fusion = (bf16[4096,2560]{1,0:T(8,128)(2,1)}, bf16[4096,2560]{1,0:T(8,128)(2,1)}, bf16[4096,2560]{1,0:T(8,128)(2,1)}) fusion(pred[4096]{0:T(1024)(128)(4,1)S(1)} %copy-done.4, f32[4096,2560]{1,0:T(8,128)} %fusion.11, f32[4096,2560]{1,0:T(8,128)} %fusion.7, bf16[1,2560,3584]{2,1,0:T(8,128)(2,1)} %param.16, ...), kind=kOutput, calls=%fused_computation.6 | convolution fusion | flops 75405197312 | bytes 194531328 | tf_op jit(solution)/shard_map/dot_general | solution.py:17
  430.7 85.4 %reduce-precision_multiply_fusion = f32[4096,3584]{1,0:T(8,128)} fusion(bf16[4096,2560]{1,0:T(8,128)(2,1)} %get-tuple-element.18, f32[4096]{0:T(1024)S(1)} %copy-done.2, bf16[1,2560,3584]{2,1,0:T(8,128)(2,1)} %param.16), kind=kOutput, calls=%fused_computation.5 | convolution fusion | flops 75191287808 | bytes 98058240 | tf_op jit(solution)/shard_map/dot_general | solution.py:13
  516.0 0.0 reduce-scatter.3.cloned.1.call-update
  516.1 0.0 reduce-scatter.5.cloned.1.call-start
  516.1 85.9 %fusion.9 = f32[4096,3584]{1,0:T(8,128)} fusion(bf16[4096,2560]{1,0:T(8,128)(2,1)} %get-tuple-element.17, bf16[1,3584,2560]{2,1,0:T(8,128)(2,1)} %param.14), kind=kOutput, calls=%fused_computation.20 | convolution fusion | flops 75161927680 | bytes 98041856 | tf_op jit(solution)/shard_map/dot_general | solution.py:17
  602.0 91.4 %add_reduce-precision_fusion = f32[4096,3584]{1,0:T(8,128)} fusion(f32[4096,3584]{1,0:T(8,128)} %fusion.9, bf16[4096,2560]{1,0:T(8,128)(2,1)} %get-tuple-element.16, bf16[1,3584,2560]{2,1,0:T(8,128)(2,1)} %param.15), kind=kOutput, calls=%fused_computation.4 | convolution fusion | flops 75191287808 | bytes 156762112 | tf_op jit(solution)/shard_map/dot_general | solution.py:17
  693.4 0.0 reduce-scatter.5.cloned.1.call-update
  693.5 0.9 slice.47
  694.4 1.0 compare_reduce_fusion
  695.4 8.0 constant_dynamic-slice_fusion
  703.4 31.8 %fusion.28 = f32[4096,640]{0,1:T(8,128)} fusion(bf16[4096,3584]{1,0:T(8,128)(2,1)} %all-gather.3.cloned.1.call-done, bf16[3584,320]{1,0:T(8,128)(2,1)S(1)} %get-tuple-element.23, bf16[3584,320]{1,0:T(8,128)(2,1)} %get-tuple-element.24), kind=kOutput, calls=%fused_computation.46 | convolution fusion | flops 18799656960 | bytes 44433408 | tf_op jit(solution)/shard_map/dot_general | solution.py:13
  735.2 21.3 %select_convert_fusion.5 = (bf16[4096,320]{0,1:T(8,128)(2,1)}, bf16[4096,320]{0,1:T(8,128)(2,1)}) fusion(f32[4096,640]{0,1:T(8,128)} %fusion.28, pred[4096]{0:T(1024)(128)(4,1)S(1)} %compare_reduce_fusion, bf16[2560,3584]{1,0:T(8,128)(2,1)} %param.19, s32[]{:T(128)S(6)} %select_n.55, bf16[4096,3584]{1,0:T(8,128)(2,1)} %all-gather.5.cloned.1.call-done, ...), kind=kOutput, calls=%fused_computation.38 | convolution fusion | flops 9460252672 | bytes 47403012 | tf_op jit(solution)/shard_map/dot_general | solution.py:17
  756.5 28.4 %fusion.22 = f32[3584,640]{0,1:T(8,128)} fusion(bf16[4096,3584]{1,0:T(8,128)(2,1)} %all-gather.3.cloned.1.call-done, bf16[4096,320]{0,1:T(8,128)(2,1)} %get-tuple-element.20, bf16[4096,320]{0,1:T(8,128)(2,1)} %get-tuple-element.19), kind=kOutput, calls=%fused_computation.32 | convolution fusion | flops 18800967680 | bytes 43778048 | tf_op jit(solution)/shard_map/dot_general | solution.py:21
  785.0 7.9 fusion.62
  792.9 0.0 copy-start.3
  792.9 21.3 %fusion.15 = f32[320,3584]{1,0:T(8,128)} fusion(bf16[4096,3584]{1,0:T(8,128)(2,1)} %all-gather.5.cloned.1.call-done, f32[4096]{0:T(1024)S(1)} %bitcast.49, f32[4096,640]{0,1:T(8,128)} %fusion.28, pred[4096]{0:T(1024)(128)(4,1)S(1)} %compare_reduce_fusion), kind=kOutput, calls=%fused_computation.24 | convolution fusion | flops 9448456192 | bytes 44453888 | tf_op jit(solution)/shard_map/dot_general | solution.py:21
  814.2 0.0 copy-done.3
  814.2 89.0 %convolution_bitcast_fusion = f32[1,2560,3584]{2,1,0:T(8,128)} fusion(bf16[4096,2560]{1,0:T(8,128)(2,1)} %get-tuple-element.18, bf16[4096,3584]{1,0:T(8,128)(2,1)} %all-gather.5.cloned.1.call-done, f32[4096]{0:T(1024)S(1)} %copy-done.3), kind=kOutput, calls=%fused_computation.11 | convolution fusion | flops 75205967872 | bytes 87048192 | tf_op jit(solution)/shard_map/dot_general | solution.py:21
  903.2 87.5 %convolution_bitcast_fusion.2 = f32[1,3584,2560]{2,1,0:T(8,128)} fusion(bf16[4096,3584]{1,0:T(8,128)(2,1)} %all-gather.3.cloned.1.call-done, bf16[4096,2560]{1,0:T(8,128)(2,1)} %get-tuple-element.17), kind=kOutput, calls=%fused_computation.13 | convolution fusion | flops 75161927680 | bytes 87031808 | tf_op jit(solution)/shard_map/dot_general | solution.py:21
  990.7 87.6 %convolution_bitcast_fusion.1 = f32[1,3584,2560]{2,1,0:T(8,128)} fusion(bf16[4096,3584]{1,0:T(8,128)(2,1)} %all-gather.3.cloned.1.call-done, bf16[4096,2560]{1,0:T(8,128)(2,1)} %get-tuple-element.16), kind=kOutput, calls=%fused_computation.12 | convolution fusion | flops 75161927680 | bytes 87031808 | tf_op jit(solution)/shard_map/dot_general | solution.py:21
  1078.3 0.0 reduce-scatter.3.cloned.1.call-done
  1078.3 8.0 add_convert_fusion.1
  1086.3 60.1 %reduce-scatter.5.cloned.1.call-done = f32[512,3584]{1,0:T(8,128)} async-done(((f32[4096,3584]{1,0:T(8,128)}), f32[512,3584]{1,0:T(8,128)}) %reduce-scatter.5.cloned.1.call-update) | async-done | bytes 7340048 | tf_op jit(solution)/shard_map/reduce_scatter | solution.py:93
  1146.4 8.0 add_convert_fusion
  (5 shorter events, 0.0 us)
Async XLA Ops:
  7.2 143.4 %all-gather.3.cloned.1.call-start = ((), (), s32[]{:S(2)}) async-start(), calls=%async_computation.2 | async-start | bytes 33030144 | tf_op jit(solution)/shard_map/all_gather | solution.py:72
  7.9 313.3 %all-gather.5.cloned.1.call-start = ((), (), s32[]{:S(2)}) async-start(), calls=%async_computation.4 | async-start | bytes 33030144 | tf_op jit(solution)/shard_map/all_gather | solution.py:73
  8.6 1069.6 %reduce-scatter.3.cloned.1.call-start = ((), (), s32[]{:S(2)}) async-start(), calls=%async_computation.3 | async-start | bytes 66060288 | tf_op jit(solution)/shard_map/reduce_scatter | solution.py:89
  26.9 17.4 %copy-start.1 = (f32[4096,18]{0,1:T(8,128)}, f32[4096,18]{0,1:T(8,128)S(1)}, u32[]{:S(2)}) copy-start(f32[4096,18]{0,1:T(8,128)S(1)} %all_gather.9) | copy-start | bytes 884740
  44.2 16.2 %copy-start = (bf16[512,3584]{1,0:T(8,128)(2,1)S(1)}, bf16[512,3584]{1,0:T(8,128)(2,1)}, u32[]{:S(2)}) copy-start(bf16[512,3584]{1,0:T(8,128)(2,1)} %param.10) | copy-start | bytes 11010052
  235.6 85.6 %copy-start.2 = (f32[4096]{0:T(1024)S(1)}, f32[4096]{0:T(1024)}, u32[]{:S(2)}) copy-start(f32[4096]{0:T(1024)} %get-tuple-element.14) | copy-start | bytes 49156
  235.6 85.6 %copy-start.4 = (pred[4096]{0:T(1024)(128)(4,1)S(1)}, pred[4096]{0:T(1024)(128)(4,1)}, u32[]{:S(2)}) copy-start(pred[4096]{0:T(1024)(128)(4,1)} %broadcast_compare_fusion) | copy-start | bytes 12292
  516.1 630.3 %reduce-scatter.5.cloned.1.call-start = ((), (), s32[]{:S(2)}) async-start(), calls=%async_computation.5 | async-start | bytes 66060288 | tf_op jit(solution)/shard_map/reduce_scatter | solution.py:93
  792.9 21.3 %copy-start.3 = (f32[4096]{0:T(1024)S(1)}, f32[4096]{0:T(1024)}, u32[]{:S(2)}) copy-start(f32[4096]{0:T(1024)} %get-tuple-element.14) | copy-start | bytes 49156
Sparse Core Ops, SparseCore 0:
  9.8 140.7 all-gather.2
  152.4 137.4 all-gather.4
  516.2 313.3 reduce-scatter.2
  833.0 313.3 reduce-scatter.4

commit v2 on v1

--- a/solution.py
+++ b/solution.py
@@ -85,7 +85,9 @@
         u_val = mm(x_all, w_gate)
         v_val = mm(x_all, w_up)
         hidden = hidden_of(u_val, v_val, keep_mine)
+        u_val, v_val, hidden = lax.optimization_barrier((u_val, v_val, hidden))
         out = g_mine * rounded(mm(hidden, w_down))
+        out, dy_all = lax.optimization_barrier((out, dy_all))
         y_sum = lax.psum_scatter(out, 'ep', scatter_dimension=0, tiled=True)
         q_mine = (g_mine * dy_all.astype(F32)).astype(BF16)
         du, dv = hidden_grads(u_val, v_val, mm_last(q_mine, w_down), keep_mine)

time: 1170 us -> 1110 us (0.949)
  waiting for transfers between devices: 73.4 us -> 3.35 us
    reduce_scatter x1, waiting for transfers between devices: 60.1 us -> 0.01 us  [local_step(): dx_sum = lax.psum_scatter(r_val, 'ep', scatter_dimension=0, tiled=True)]
    dot_general x7, matrix products: 339 us -> 356 us  [mm(): return jnp.dot(a, b, preferred_element_type=F32)]
  transfers between devices with their start and end apart: 4 -> 4, of which waited for: 2 -> 1; matrix products, arithmetic and copies ran while one was open for 74% -> 96% of each run, Pallas kernels for 0% -> 0%
where the time goes in v2:
time: 1110 us
  matrix products  1030 us (93%)
  other arithmetic  21.2 us (2%)
  local copies, waits for them, and re-layouts  18.2 us (2%)
  blocking collectives  17.2 us (2%)
  between operations  14 us (1%)
    dot_general x7, matrix products, mm_last(): return lax.dot_general(a, b, CONTRACT_LAST, preferred_element_type=F32)  363 us
    dot_general x7, matrix products, mm(): return jnp.dot(a, b, preferred_element_type=F32)  356 us
    dot_general x5, matrix products, mm_first(): return lax.dot_general(a, b, CONTRACT_FIRST, preferred_element_type=F32)  314 us
  transfers between devices with their start and end apart: 4, of which 1 were waited for; matrix products, arithmetic and copies ran while one was open for 96% of the time, Pallas kernels for 0%

profile of v2, /device:TPU:0, one launch (start us, length us, event | category | flops | bytes accessed | tf_op | source)
XLA Modules:
  0.0 1107.3 jit_solution(3145096331143597379)
XLA Ops:
  7.2 0.0 all-gather.3.cloned.1.call-start
  7.2 0.7 all-gather.3.cloned.1.call-update
  7.9 0.0 all-gather.5.cloned.1.call-start
  7.9 0.7 all-gather.5.cloned.1.call-update
  8.6 0.0 reduce-scatter.3.cloned.1.call-start
  8.7 0.8 fusion.49
  9.5 0.6 convert_element_type.56
  10.1 0.7 convert_element_type.55
  10.8 0.8 select_reduce_fusion
  11.6 0.0 copy-start.3
  11.6 0.6 copy-done.3
  12.2 0.0 copy-start
  12.2 16.1 %fusion.63 = f32[512,2560]{1,0:T(8,128)} fusion(bf16[512,3584]{1,0:T(8,128)(2,1)} %param.10, bf16[3584,2560]{1,0:T(8,128)(2,1)} %param.18), kind=kOutput, calls=%fused_computation.89 | convolution fusion | flops 9395240960 | bytes 27262976 | tf_op jit(solution)/shard_map/dot_general | solution.py:13
  28.3 0.0 copy-done
  28.3 0.0 copy-start.1
  28.3 15.0 %fusion.62 = f32[512,2560]{1,0:T(8,128)} fusion(bf16[512,3584]{1,0:T(8,128)(2,1)S(1)} %copy-done, bf16[3584,2560]{1,0:T(8,128)(2,1)} %param.17), kind=kOutput, calls=%fused_computation.88 | convolution fusion | flops 9395240960 | bytes 27262976 | tf_op jit(solution)/shard_map/dot_general | solution.py:13
  43.4 0.0 copy-done.1
  43.4 15.0 %fusion.31 = f32[512,2560]{1,0:T(8,128)} fusion(bf16[2560,3584]{1,0:T(8,128)(2,1)} %param.19, bf16[512,3584]{1,0:T(8,128)(2,1)S(1)} %copy-done.1, f32[512]{0:T(512)S(1)} %bitcast.52), kind=kOutput, calls=%fused_computation.49 | convolution fusion | flops 9400745984 | bytes 27265024 | tf_op jit(solution)/shard_map/dot_general | solution.py:17
  58.4 29.7 %reduce-precision_multiply_fusion.1 = f32[512,3584]{1,0:T(8,128)} fusion(bf16[2560,3584]{1,0:T(8,128)(2,1)} %param.19, f32[512]{0:T(512)S(1)} %bitcast.53, f32[512,2560]{1,0:T(8,128)} %fusion.63, pred[512]{0:T(512)(128)(4,1)S(1)} %slice_reduce_fusion, f32[512,2560]{1,0:T(8,128)} %fusion.62), kind=kOutput, calls=%fused_computation.29 | convolution fusion | flops 9408086016 | bytes 36178432 | tf_op jit(solution)/shard_map/dot_general | solution.py:13
  88.1 22.5 %fusion.33 = f32[512,3584]{1,0:T(8,128)} fusion(bf16[3584,2560]{1,0:T(8,128)(2,1)} %param.17, f32[512,2560]{1,0:T(8,128)} %fusion.62, f32[512,2560]{1,0:T(8,128)} %fusion.63, f32[512,2560]{1,0:T(8,128)} %fusion.31, pred[512]{0:T(512)(128)(4,1)S(1)} %slice_reduce_fusion), kind=kOutput, calls=%fused_computation.51 | convolution fusion | flops 9410969600 | bytes 41419264 | tf_op jit(solution)/shard_map/dot_general | solution.py:17
  110.6 0.0 copy-start.4
  110.6 0.0 copy-start.5
  110.6 21.0 %add_reduce-precision_fusion.1 = f32[512,3584]{1,0:T(8,128)} fusion(f32[512,3584]{1,0:T(8,128)} %fusion.33, bf16[3584,2560]{1,0:T(8,128)(2,1)} %param.18, f32[512,2560]{1,0:T(8,128)} %fusion.31, pred[512]{0:T(512)(128)(4,1)S(1)} %slice_reduce_fusion, f32[512,2560]{1,0:T(8,128)} %fusion.62), kind=kOutput, calls=%fused_computation.27 | convolution fusion | flops 9409396736 | bytes 43516416 | tf_op jit(solution)/shard_map/dot_general | solution.py:17
  131.6 0.0 copy-done.4
  131.6 0.0 copy-done.5
  131.6 17.2 %all_gather.9 = f32[4096,18]{0,1:T(8,128)S(1)} all-gather(f32[512,18]{0,1:T(8,128)S(1)} %pad_maximum_fusion), channel_id=1, replica_groups=mesh['ep'=8] {'ep'}, dimensions={0}, use_global_device_ids=true | all-gather | bytes 331776 | tf_op jit(solution)/shard_map/all_gather | solution.py:64
  148.9 0.0 copy-start.2
  148.9 0.8 fusion.48
  149.7 0.6 broadcast_compare_fusion
  150.2 1.9 all-gather.3.cloned.1.call-done
  152.2 0.0 copy-start.8
  152.2 85.3 %fusion.10 = f32[4096,2560]{1,0:T(8,128)} fusion(bf16[4096,3584]{1,0:T(8,128)(2,1)} %all-gather.3.cloned.1.call-done, bf16[1,3584,2560]{2,1,0:T(8,128)(2,1)} %param.14), kind=kOutput, calls=%fused_computation.21 | convolution fusion | flops 75161927680 | bytes 89653248 | tf_op jit(solution)/shard_map/dot_general | solution.py:13
  237.5 0.0 copy-done.2
  237.5 0.0 copy-done.8
  237.5 0.0 copy-start.6
  237.5 92.2 %select_convert_fusion.2 = (bf16[4096,2560]{1,0:T(8,128)(2,1)}, f32[4096,2560]{1,0:T(8,128)}) fusion(f32[4096,2560]{1,0:T(8,128)} %fusion.10, pred[4096]{0:T(1024)(128)(4,1)S(1)} %copy-done.8, bf16[4096,3584]{1,0:T(8,128)(2,1)} %all-gather.3.cloned.1.call-done, bf16[1,3584,2560]{2,1,0:T(8,128)(2,1)} %param.15), kind=kOutput, calls=%fused_computation.9 | convolution fusion | flops 75235328000 | bytes 152571904 | tf_op jit(solution)/shard_map/dot_general | solution.py:13
  329.7 0.0 copy-done.6
  329.7 85.7 %reduce-precision_multiply_fusion = f32[4096,3584]{1,0:T(8,128)} fusion(bf16[4096,2560]{1,0:T(8,128)(2,1)} %get-tuple-element.17, f32[4096]{0:T(1024)S(1)} %copy-done.6, bf16[1,2560,3584]{2,1,0:T(8,128)(2,1)} %param.16), kind=kOutput, calls=%fused_computation.5 | convolution fusion | flops 75191287808 | bytes 98058240 | tf_op jit(solution)/shard_map/dot_general | solution.py:13
  415.4 0.0 copy-start.9
  415.4 0.0 all-gather.5.cloned.1.call-done
  415.4 0.0 reduce-scatter.3.cloned.1.call-update
  415.5 0.0 reduce-scatter.5.cloned.1.call-start
  415.5 0.6 copy-done.9
  416.1 106.0 %select_convert_fusion = (bf16[4096,2560]{1,0:T(8,128)(2,1)}, bf16[4096,2560]{1,0:T(8,128)(2,1)}) fusion(f32[4096,2560]{1,0:T(8,128)} %fusion.10, pred[4096]{0:T(1024)(128)(4,1)S(1)} %copy-done.9, f32[4096,2560]{1,0:T(8,128)} %get-tuple-element.21, bf16[1,2560,3584]{2,1,0:T(8,128)(2,1)} %param.16, bf16[4096,3584]{1,0:T(8,128)(2,1)} %all-gather.5.cloned.1.call-done, ...), kind=kOutput, calls=%fused_computation.6 | convolution fusion | flops 75373740032 | bytes 173559808 | tf_op jit(solution)/shard_map/dot_general | solution.py:17
  522.1 85.7 %fusion.8 = f32[4096,3584]{1,0:T(8,128)} fusion(bf16[4096,2560]{1,0:T(8,128)(2,1)} %get-tuple-element.27, bf16[1,3584,2560]{2,1,0:T(8,128)(2,1)} %param.14), kind=kOutput, calls=%fused_computation.19 | convolution fusion | flops 75161927680 | bytes 98041856 | tf_op jit(solution)/shard_map/dot_general | solution.py:17
  607.8 91.7 %add_reduce-precision_fusion = f32[4096,3584]{1,0:T(8,128)} fusion(f32[4096,3584]{1,0:T(8,128)} %fusion.8, bf16[4096,2560]{1,0:T(8,128)(2,1)} %get-tuple-element.26, bf16[1,3584,2560]{2,1,0:T(8,128)(2,1)} %param.15), kind=kOutput, calls=%fused_computation.4 | convolution fusion | flops 75191287808 | bytes 156762112 | tf_op jit(solution)/shard_map/dot_general | solution.py:17
  699.5 0.0 reduce-scatter.5.cloned.1.call-update
  699.5 0.9 slice.47
  700.4 1.0 compare_reduce_fusion
  701.4 8.0 constant_dynamic-slice_fusion
  709.4 32.0 %fusion.27 = f32[4096,640]{0,1:T(8,128)} fusion(bf16[4096,3584]{1,0:T(8,128)(2,1)} %all-gather.3.cloned.1.call-done, bf16[3584,320]{1,0:T(8,128)(2,1)S(1)} %get-tuple-element.34, bf16[3584,320]{1,0:T(8,128)(2,1)} %get-tuple-element.35), kind=kOutput, calls=%fused_computation.45 | convolution fusion | flops 18799656960 | bytes 44433408 | tf_op jit(solution)/shard_map/dot_general | solution.py:13
  741.5 21.3 %select_convert_fusion.5 = (bf16[4096,320]{0,1:T(8,128)(2,1)}, bf16[4096,320]{0,1:T(8,128)(2,1)}) fusion(f32[4096,640]{0,1:T(8,128)} %fusion.27, pred[4096]{0:T(1024)(128)(4,1)S(1)} %compare_reduce_fusion, bf16[2560,3584]{1,0:T(8,128)(2,1)} %param.19, s32[]{:T(128)S(6)} %select_n.55, bf16[4096,3584]{1,0:T(8,128)(2,1)} %all-gather.5.cloned.1.call-done, ...), kind=kOutput, calls=%fused_computation.37 | convolution fusion | flops 9460252672 | bytes 47403012 | tf_op jit(solution)/shard_map/dot_general | solution.py:17
  762.8 28.2 %fusion.21 = f32[3584,640]{0,1:T(8,128)} fusion(bf16[4096,3584]{1,0:T(8,128)(2,1)} %all-gather.3.cloned.1.call-done, bf16[4096,320]{0,1:T(8,128)(2,1)} %get-tuple-element.29, bf16[4096,320]{0,1:T(8,128)(2,1)} %get-tuple-element.28), kind=kOutput, calls=%fused_computation.31 | convolution fusion | flops 18800967680 | bytes 43778048 | tf_op jit(solution)/shard_map/dot_general | solution.py:21
  791.0 7.9 fusion.61
  798.9 0.0 copy-start.7
  798.9 21.3 %fusion.14 = f32[320,3584]{1,0:T(8,128)} fusion(bf16[4096,3584]{1,0:T(8,128)(2,1)} %all-gather.5.cloned.1.call-done, f32[4096]{0:T(1024)S(1)} %bitcast.51, f32[4096,640]{0,1:T(8,128)} %fusion.27, pred[4096]{0:T(1024)(128)(4,1)S(1)} %compare_reduce_fusion), kind=kOutput, calls=%fused_computation.23 | convolution fusion | flops 9448456192 | bytes 44453888 | tf_op jit(solution)/shard_map/dot_general | solution.py:21
  820.2 0.0 copy-done.7
  820.2 89.0 %convolution_bitcast_fusion = f32[1,2560,3584]{2,1,0:T(8,128)} fusion(bf16[4096,2560]{1,0:T(8,128)(2,1)} %get-tuple-element.17, bf16[4096,3584]{1,0:T(8,128)(2,1)} %all-gather.5.cloned.1.call-done, f32[4096]{0:T(1024)S(1)} %copy-done.7), kind=kOutput, calls=%fused_computation.10 | convolution fusion | flops 75205967872 | bytes 87048192 | tf_op jit(solution)/shard_map/dot_general | solution.py:21
  909.2 87.8 %convolution_bitcast_fusion.2 = f32[1,3584,2560]{2,1,0:T(8,128)} fusion(bf16[4096,3584]{1,0:T(8,128)(2,1)} %all-gather.3.cloned.1.call-done, bf16[4096,2560]{1,0:T(8,128)(2,1)} %get-tuple-element.27), kind=kOutput, calls=%fused_computation.12 | convolution fusion | flops 75161927680 | bytes 87031808 | tf_op jit(solution)/shard_map/dot_general | solution.py:21
  997.0 87.6 %convolution_bitcast_fusion.1 = f32[1,3584,2560]{2,1,0:T(8,128)} fusion(bf16[4096,3584]{1,0:T(8,128)(2,1)} %all-gather.3.cloned.1.call-done, bf16[4096,2560]{1,0:T(8,128)(2,1)} %get-tuple-element.26), kind=kOutput, calls=%fused_computation.11 | convolution fusion | flops 75161927680 | bytes 87031808 | tf_op jit(solution)/shard_map/dot_general | solution.py:21
  1084.6 0.0 reduce-scatter.3.cloned.1.call-done
  1084.6 8.0 add_convert_fusion.1
  1092.6 0.0 reduce-scatter.5.cloned.1.call-done
  1092.6 8.0 add_convert_fusion
  (4 shorter events, 0.0 us)
Async XLA Ops:
  7.2 145.0 %all-gather.3.cloned.1.call-start = ((), (), s32[]{:S(2)}) async-start(), calls=%async_computation.2 | async-start | bytes 33030144 | tf_op jit(solution)/shard_map/all_gather | solution.py:72
  7.9 407.5 %all-gather.5.cloned.1.call-start = ((), (), s32[]{:S(2)}) async-start(), calls=%async_computation.3 | async-start | bytes 33030144 | tf_op jit(solution)/shard_map/all_gather | solution.py:73
  8.6 1075.9 %reduce-scatter.3.cloned.1.call-start = ((), (), s32[]{:S(2)}) async-start(), calls=%async_computation.4 | async-start | bytes 66060288 | tf_op jit(solution)/shard_map/reduce_scatter | solution.py:91
  11.6 0.6 copy-start.3
  12.2 16.1 %copy-start = (bf16[512,3584]{1,0:T(8,128)(2,1)S(1)}, bf16[512,3584]{1,0:T(8,128)(2,1)}, u32[]{:S(2)}) copy-start(bf16[512,3584]{1,0:T(8,128)(2,1)} %param.10) | copy-start | bytes 11010052
  28.3 15.1 %copy-start.1 = (bf16[512,3584]{1,0:T(8,128)(2,1)S(1)}, bf16[512,3584]{1,0:T(8,128)(2,1)}, u32[]{:S(2)}) copy-start(bf16[512,3584]{1,0:T(8,128)(2,1)} %param.13) | copy-start | bytes 11010052
  110.6 21.0 %copy-start.4 = (f32[512,9]{0,1:T(8,128)S(1)}, f32[512,9]{0,1:T(8,128)}, u32[]{:S(2)}) copy-start(f32[512,9]{0,1:T(8,128)} %copy-done.3) | copy-start | bytes 55300
  110.6 21.0 %copy-start.5 = (f32[512,9]{0,1:T(8,128)S(1)}, f32[512,9]{0,1:T(8,128)}, u32[]{:S(2)}) copy-start(f32[512,9]{0,1:T(8,128)} %convert_element_type.56) | copy-start | bytes 55300
  148.9 88.6 %copy-start.2 = (f32[4096,18]{0,1:T(8,128)}, f32[4096,18]{0,1:T(8,128)S(1)}, u32[]{:S(2)}) copy-start(f32[4096,18]{0,1:T(8,128)S(1)} %all_gather.9) | copy-start | bytes 884740
  152.2 85.3 %copy-start.8 = (pred[4096]{0:T(1024)(128)(4,1)S(1)}, pred[4096]{0:T(1024)(128)(4,1)}, u32[]{:S(2)}) copy-start(pred[4096]{0:T(1024)(128)(4,1)} %broadcast_compare_fusion) | copy-start | bytes 12292
  237.5 92.2 %copy-start.6 = (f32[4096]{0:T(1024)S(1)}, f32[4096]{0:T(1024)}, u32[]{:S(2)}) copy-start(f32[4096]{0:T(1024)} %get-tuple-element.24) | copy-start | bytes 49156
  415.4 0.7 copy-start.9
  415.5 677.1 %reduce-scatter.5.cloned.1.call-start = ((), (), s32[]{:S(2)}) async-start(), calls=%async_computation.5 | async-start | bytes 66060288 | tf_op jit(solution)/shard_map/reduce_scatter | solution.py:95
  798.9 21.3 %copy-start.7 = (f32[4096]{0:T(1024)S(1)}, f32[4096]{0:T(1024)}, u32[]{:S(2)}) copy-start(f32[4096]{0:T(1024)} %get-tuple-element.24) | copy-start | bytes 49156
Sparse Core Ops, SparseCore 0:
  9.8 142.3 all-gather.2
  154.0 137.4 all-gather.4
  415.6 313.3 reduce-scatter.2
  732.3 313.3 reduce-scatter.4
